TPU v7x, 32 devices: a whole 2x2x4 slice. The times are simulated.
32 devices in a mesh: tp: 2 (over x), dp: 4 (over z), dq: 4 (over y, core).
Axes of the slice: x: 2, y: 2, z: 4, core: 2. Of those that a mesh axis runs over, the one named last changes fastest.
Arguments:
- tokens: bfloat16 [16, 512, 768], P(('dp', 'dq')), may hold values from -6 to 6
- lengths: int32 [16], P(('dp', 'dq')), may hold values from 10 to 512, as said below
- weight_qkv: bfloat16 [768, 3, 768], P(None, None, 'tp'), may hold values from -0.21875 to 0.21875
- weight_out: bfloat16 [768, 768], P('tp'), may hold values from -0.875 to 0.875
- gain_one: float32 [768], replicated, may hold values from 0.25 to 1.75
- bias_one: float32 [768], replicated, may hold values from -3 to 3
- weight_up: bfloat16 [768, 3072], P(None, 'tp'), may hold values from -0.21875 to 0.21875
- weight_down: bfloat16 [3072, 768], P('tp'), may hold values from -0.15625 to 0.15625
- gain_two: float32 [768], replicated, may hold values from 0.25 to 1.75
- bias_two: float32 [768], replicated, may hold values from -3 to 3
- cotangent: bfloat16 [16, 512, 768], P(('dp', 'dq')), may hold values from -6 to 6
Outputs:
- layer_out: bfloat16 [16, 512, 768], P(('dp', 'dq'))
- grad_tokens: bfloat16 [16, 512, 768], P(('dp', 'dq'))
- grad_weight_qkv: float32 [768, 3, 768], P(None, None, 'tp')
- grad_weight_out: float32 [768, 768], P('tp')
- grad_gain_one: float32 [768], replicated
- grad_bias_one: float32 [768], replicated
- grad_weight_up: float32 [768, 3072], P(None, 'tp')
- grad_weight_down: float32 [3072, 768], P('tp')
- grad_gain_two: float32 [768], replicated
- grad_bias_two: float32 [768], replicated
Inputs may be any that keep to these rules, and one draw needn't show every extreme that they name: `lengths`: real tokens of each pair; its rows from that count to 512 are padding keys. Heavy-tailed: most pairs are short; some pair has exactly 512 and some exactly 10.
All inputs are finite; a program needn't handle non-finite values.
Results may differ from a plain program's by a relative error of at most 0.018.
Values may be sent and summed in bfloat16 or wider, within the bound.
A program may use at most 128 MiB of HBM per device.

v0:
```python
import jax
import jax.numpy as jnp
from jax import lax
from jax.sharding import PartitionSpec as P

HEAD_DIM = 64


epsilon = 1e-05


def gelu_exact(values):
    return 0.5 * values * (1.0 + lax.erf(values * 0.7071067811865476))


def contract_rows(left, right):
    return lax.dot_general(
        left, right, (((0,), (0,)), ((), ())), preferred_element_type=jnp.float32
    )


def contract_cols(left, right):
    return lax.dot_general(
        left, right, (((1,), (1,)), ((), ())), preferred_element_type=jnp.float32
    )


def norm_forward(values, gain_vec, bias_vec):
    centred = values - jnp.mean(values, axis=-1, keepdims=True)
    inverse = lax.rsqrt(jnp.mean(centred * centred, axis=-1, keepdims=True) + epsilon)
    unit = centred * inverse
    return (unit * gain_vec + bias_vec, unit, inverse)


def norm_backward(grad_out, unit, inverse, gain_vec):
    scaled = grad_out * gain_vec
    centre = jnp.mean(scaled, axis=-1, keepdims=True)
    along = jnp.mean(scaled * unit, axis=-1, keepdims=True)
    return inverse * (scaled - centre - unit * along)


def masked_scores(queries, key_rows, length, scaling):
    scores = (
        jnp.einsum("qhe,khe->hqk", queries, key_rows, preferred_element_type=jnp.float32) * scaling
    )
    key_live = jnp.arange(key_rows.shape[0], dtype=jnp.int32) < length
    return jnp.where(key_live[None, None, :], scores, -1000000000.0)


def attend_forward(packed_seq, length, scaling):
    queries = packed_seq[:, 0]
    key_rows = packed_seq[:, 1]
    val_rows = packed_seq[:, 2]
    scores = masked_scores(queries, key_rows, length, scaling)
    top = jnp.max(scores, axis=-1, keepdims=True)
    expsum = jnp.sum(jnp.exp(scores - top), axis=-1, keepdims=True)
    log_total = top + jnp.log(expsum)
    probs_low = jnp.exp(scores - log_total).astype(jnp.bfloat16)
    attended = jnp.einsum("hqk,khe->qhe", probs_low, val_rows, preferred_element_type=jnp.float32)
    return (attended.astype(jnp.bfloat16), log_total)


def attend_backward(packed_seq, length, log_total, grad_att, scaling):
    queries = packed_seq[:, 0]
    key_rows = packed_seq[:, 1]
    val_rows = packed_seq[:, 2]
    scores = masked_scores(queries, key_rows, length, scaling)
    probs = jnp.exp(scores - log_total)
    probs_low = probs.astype(jnp.bfloat16)
    grad_values = jnp.einsum(
        "hqk,qhe->khe", probs_low, grad_att, preferred_element_type=jnp.float32
    )
    grad_probs = jnp.einsum("qhe,khe->hqk", grad_att, val_rows, preferred_element_type=jnp.float32)
    centre = jnp.sum(probs * grad_probs, axis=-1, keepdims=True)
    grad_scores = (probs * (grad_probs - centre)).astype(jnp.bfloat16)
    grad_queries = (
        jnp.einsum("hqk,khe->qhe", grad_scores, key_rows, preferred_element_type=jnp.float32)
        * scaling
    )
    grad_keys = (
        jnp.einsum("hqk,qhe->khe", grad_scores, queries, preferred_element_type=jnp.float32)
        * scaling
    )
    return jnp.stack([grad_queries, grad_keys, grad_values], axis=1).astype(jnp.bfloat16)


def on_device(
    tokens,
    lengths,
    weight_qkv,
    weight_out,
    gain_one,
    bias_one,
    weight_up,
    weight_down,
    gain_two,
    bias_two,
    cotangent,
):
    seq_count, seq_len, width = tokens.shape
    local_cols = weight_qkv.shape[2]
    head_local = local_cols // HEAD_DIM
    scaling = HEAD_DIM ** (-0.5)
    token_rows = tokens.reshape(-1, width)
    total_rows = token_rows.shape[0]
    share_rows = total_rows // lax.axis_size("tp")
    share_start = lax.axis_index("tp") * share_rows
    token_share = lax.dynamic_slice_in_dim(token_rows, share_start, share_rows, 0).astype(
        jnp.float32
    )
    cot_rows = cotangent.reshape(-1, width)
    grad_output = lax.dynamic_slice_in_dim(cot_rows, share_start, share_rows, 0).astype(jnp.float32)
    qkv_matrix = weight_qkv.reshape(width, 3 * local_cols)
    packed = jnp.dot(token_rows, qkv_matrix, preferred_element_type=jnp.float32).astype(
        jnp.bfloat16
    )
    packed = packed.reshape(seq_count, seq_len, 3, head_local, HEAD_DIM)
    attended, log_total = lax.map(
        lambda element: attend_forward(element[0], element[1], scaling), (packed, lengths)
    )
    attended_rows = attended.reshape(-1, local_cols)
    branch = lax.psum_scatter(
        jnp.dot(attended_rows, weight_out, preferred_element_type=jnp.float32).astype(jnp.bfloat16),
        "tp",
        scatter_dimension=0,
        tiled=True,
    ).astype(jnp.float32)
    normed, unit_one, inverse_one = norm_forward(token_share + branch, gain_one, bias_one)
    normed_low = lax.all_gather(normed.astype(jnp.bfloat16), "tp", axis=0, tiled=True)
    upward = jnp.dot(normed_low, weight_up, preferred_element_type=jnp.float32)
    activated = gelu_exact(upward).astype(jnp.bfloat16)
    downward = lax.psum_scatter(
        jnp.dot(activated, weight_down, preferred_element_type=jnp.float32).astype(jnp.bfloat16),
        "tp",
        scatter_dimension=0,
        tiled=True,
    ).astype(jnp.float32)
    output, unit_two, inverse_two = norm_forward(normed + downward, gain_two, bias_two)
    part_gain_two = jnp.sum(grad_output * unit_two, axis=0)
    part_bias_two = jnp.sum(grad_output, axis=0)
    grad_res_two = norm_backward(grad_output, unit_two, inverse_two, gain_two)
    grad_down_in = lax.all_gather(grad_res_two.astype(jnp.bfloat16), "tp", axis=0, tiled=True)
    grad_weight_down = contract_rows(activated, grad_down_in)
    grad_act = contract_cols(grad_down_in, weight_down)
    gelu_value, gelu_pull = jax.vjp(gelu_exact, upward)
    grad_up_in = gelu_pull(grad_act)[0].astype(jnp.bfloat16)
    grad_weight_up = contract_rows(normed_low, grad_up_in)
    grad_normed = grad_res_two + lax.psum_scatter(
        contract_cols(grad_up_in, weight_up).astype(jnp.bfloat16),
        "tp",
        scatter_dimension=0,
        tiled=True,
    ).astype(jnp.float32)
    part_gain_one = jnp.sum(grad_normed * unit_one, axis=0)
    part_bias_one = jnp.sum(grad_normed, axis=0)
    grad_res_one = norm_backward(grad_normed, unit_one, inverse_one, gain_one)
    grad_branch = lax.all_gather(grad_res_one.astype(jnp.bfloat16), "tp", axis=0, tiled=True)
    grad_weight_out = contract_rows(attended_rows, grad_branch)
    grad_attended = contract_cols(grad_branch, weight_out).astype(jnp.bfloat16)
    grad_attended = grad_attended.reshape(seq_count, seq_len, head_local, HEAD_DIM)
    grad_packed = lax.map(
        lambda element: attend_backward(element[0], element[1], element[2], element[3], scaling),
        (packed, lengths, log_total, grad_attended),
    )
    grad_packed = grad_packed.reshape(-1, 3 * local_cols)
    grad_weight_qkv = contract_rows(token_rows, grad_packed).reshape(width, 3, local_cols)
    grad_input = grad_res_one + lax.psum_scatter(
        contract_cols(grad_packed, qkv_matrix).astype(jnp.bfloat16),
        "tp",
        scatter_dimension=0,
        tiled=True,
    ).astype(jnp.float32)
    out_rows, grad_in_rows = (
        lax.all_gather(output.astype(jnp.bfloat16), "tp", axis=0, tiled=True),
        lax.all_gather(grad_input.astype(jnp.bfloat16), "tp", axis=0, tiled=True),
    )
    grad_gain_one, grad_bias_one, grad_gain_two, grad_bias_two = lax.psum(
        (part_gain_one, part_bias_one, part_gain_two, part_bias_two), "tp"
    )
    pieces = (
        grad_weight_qkv,
        grad_weight_out,
        grad_gain_one,
        grad_bias_one,
        grad_weight_up,
        grad_weight_down,
        grad_gain_two,
        grad_bias_two,
    )
    flat = jnp.concatenate([member.reshape(-1) for member in pieces])
    reduced = lax.psum_scatter(flat, ("dp", "dq"), scatter_dimension=0, tiled=True)
    summed = lax.all_gather(reduced.astype(jnp.bfloat16), ("dp", "dq"), axis=0, tiled=True).astype(
        reduced.dtype
    )
    results = []
    start_at = 0
    for member in pieces:
        extent = member.size
        results.append(summed[start_at : start_at + extent].reshape(member.shape))
        start_at += extent
    layer_out = out_rows.reshape(seq_count, seq_len, width)
    grad_tokens = grad_in_rows.reshape(seq_count, seq_len, width)
    return (
        layer_out,
        grad_tokens,
        results[0],
        results[1],
        results[2],
        results[3],
        results[4],
        results[5],
        results[6],
        results[7],
    )


def solution(mesh):
    return jax.shard_map(
        on_device,
        mesh=mesh,
        in_specs=(
            P(("dp", "dq"), None, None),
            P(("dp", "dq")),
            P(None, None, "tp"),
            P("tp", None),
            P(),
            P(),
            P(None, "tp"),
            P("tp", None),
            P(),
            P(),
            P(("dp", "dq"), None, None),
        ),
        out_specs=(
            P(("dp", "dq"), None, None),
            P(("dp", "dq"), None, None),
            P(None, None, "tp"),
            P("tp", None),
            P(),
            P(),
            P(None, "tp"),
            P("tp", None),
            P(),
            P(),
        ),
        check_vma=False,
    )
```

profile of v0, /device:TPU:0, one launch (start us, length us, event | category | flops | bytes accessed | tf_op | source)
XLA Modules:
  0.0 789.6 jit_solution(17417523677403604473)
XLA Ops:
  7.2 4.0 copy.36
  11.3 3.7 convolution_convert_fusion
  15.0 2.4 copy.37
  18.1 2.6 fusion
  24.8 1.7 copy-done.3
  26.5 1.7 convolution_convert_fusion.7
  28.9 1.5 convolution_convert_fusion.4
  30.5 20.3 %reduce-scatter.5.cloned.1.call-done = bf16[256,768]{1,0:T(8,128)(2,1)} async-done(((bf16[512,768]{1,0:T(8,128)(2,1)}), bf16[256,768]{1,0:T(8,128)(2,1)}) %reduce-scatter.5.cloned.1.call-update) | async-done | bytes 393232 | tf_op jit(solution)/shard_map/reduce_scatter | solution.py:122
  54.5 11.4 %all_gather.18 = bf16[512,768]{1,0:T(8,128)(2,1)S(1)} all-gather(bf16[256,768]{1,0:T(8,128)(2,1)S(1)} %fusion.21), channel_id=1, replica_groups=mesh['tp'=2,'dp'=4,'dq'=4] {'tp'}, dimensions={0}, use_global_device_ids=true | all-gather | bytes 1179648 | tf_op jit(solution)/shard_map/all_gather | solution.py:129
  65.9 2.8 multiply_convert_fusion.1
  69.9 2.3 convolution_convert_fusion.2
  72.2 17.6 %reduce-scatter.7.cloned.1.call-done = bf16[256,768]{1,0:T(8,128)(2,1)} async-done(((bf16[512,768]{1,0:T(8,128)(2,1)}), bf16[256,768]{1,0:T(8,128)(2,1)}) %reduce-scatter.7.cloned.1.call-update) | async-done | bytes 393232 | tf_op jit(solution)/shard_map/reduce_scatter | solution.py:132
  91.6 2.2 fusion.15
  95.1 11.5 %all_gather.20 = bf16[512,768]{1,0:T(8,128)(2,1)S(1)} all-gather(bf16[256,768]{1,0:T(8,128)(2,1)S(1)} %get-tuple-element.76), channel_id=1, replica_groups=mesh['tp'=2,'dp'=4,'dq'=4] {'tp'}, dimensions={0}, use_global_device_ids=true | all-gather | bytes 1179648 | tf_op jit(solution)/shard_map/all_gather | solution.py:142
  106.7 2.4 add_convert_fusion
  110.2 2.3 convolution_convert_fusion.1
  115.2 1.7 convert_reduce_fusion
  116.9 5.3 fusion.33
  122.1 5.8 reshape.165
  127.9 3.6 fusion.34
  131.6 5.8 reshape.166
  137.4 2.1 multiply_reduce_fusion.1
  139.5 2.3 fusion.25
  141.9 10.4 %all_gather.21 = bf16[512,768]{1,0:T(8,128)(2,1)S(1)} all-gather(bf16[256,768]{1,0:T(8,128)(2,1)S(1)} %get-tuple-element.74), channel_id=1, replica_groups=mesh['tp'=2,'dp'=4,'dq'=4] {'tp'}, dimensions={0}, use_global_device_ids=true | all-gather | bytes 1179648 | tf_op jit(solution)/shard_map/all_gather | solution.py:157
  152.8 4.5 multiply_reduce_fusion
  157.5 2.2 multiply_convert_fusion
  163.3 2.9 convolution_bitcast_fusion
  166.2 2.1 convolution_convert_fusion.3
  168.3 5.2 copy.42
  173.4 4.5 reshape_reshape.3
  178.0 4.0 constant_dynamic-update-slice_fusion.5
  183.2 7.3 all-reduce.2
  193.1 41.0 %dynamic-update-slice.5 = f32[3542016]{0:T(1024)} dynamic-update-slice(f32[3542016]{0:T(1024)} %constant_dynamic-update-slice_fusion.2, f32[1179648]{0:T(1024)} %reshape.165, s32[]{} %constant.95) | dynamic-update-slice | bytes 9437188
  234.1 40.8 %dynamic-update-slice.6 = f32[3542016]{0:T(1024)} dynamic-update-slice(f32[3542016]{0:T(1024)} %dynamic-update-slice.5, f32[1179648]{0:T(1024)} %reshape.166, s32[]{} %constant.96) | dynamic-update-slice | bytes 9437188
  277.5 297.1 %all-reduce.7 = bf16[3542016]{0:T(1024)(128)(2,1)} all-reduce(f32[3542016]{0:T(1024)} %constant_dynamic-update-slice_fusion), channel_id=6, replica_groups=mesh['tp'=2,'dp'=4,'dq'=4] {'dp','dq'}, use_global_device_ids=true, to_apply=%region_23.24.clone | all-reduce | flops 3542016 | bytes 21252096
  575.9 3.4 broadcast.103
  579.3 7.6 dynamic-update-slice
  587.9 9.8 %all_gather.19 = bf16[512,768]{1,0:T(8,128)(2,1)} all-gather(bf16[256,768]{1,0:T(8,128)(2,1)S(1)} %copy-done.20), channel_id=1, replica_groups=mesh['tp'=2,'dp'=4,'dq'=4] {'tp'}, dimensions={0}, use_global_device_ids=true | all-gather | bytes 1179648 | tf_op jit(solution)/shard_map/all_gather | solution.py:174
  598.7 10.9 %all_gather.22 = bf16[512,768]{1,0:T(8,128)(2,1)} all-gather(bf16[256,768]{1,0:T(8,128)(2,1)S(1)} %add_convert_fusion.1), channel_id=1, replica_groups=mesh['tp'=2,'dp'=4,'dq'=4] {'tp'}, dimensions={0}, use_global_device_ids=true | all-gather | bytes 1179648 | tf_op jit(solution)/shard_map/all_gather | solution.py:175
  609.6 133.7 %all-reduce.6.cloned.1.call-done = bf16[3542016]{0:T(1024)(128)(2,1)} async-done(((bf16[3542016]{0:T(1024)(128)(2,1)}), bf16[3542016]{0:T(1024)(128)(2,1)}) %all-reduce.6.cloned.1.call-update) | async-done | bytes 7084048
  743.3 5.8 fusion.30
  749.1 5.8 slice.81
  754.9 6.0 slice.83
  760.9 3.5 slice.89
  764.3 6.3 reshape.167
  770.7 4.4 copy.43
  779.0 2.1 copy.62
  781.0 2.1 copy.63
  (133 shorter events, 33.3 us)
Async XLA Ops:
  7.2 58.7 %copy-start = (bf16[768,1536]{1,0:T(8,128)(2,1)S(1)}, bf16[768,1536]{1,0:T(8,128)(2,1)}, u32[]{:S(2)}) copy-start(bf16[768,1536]{1,0:T(8,128)(2,1)} %param.17) | copy-start | bytes 7077892
  7.2 4.1 copy-start.6
  7.2 43.6 %reduce-scatter.5.cloned.1.call-start = ((), (), s32[]{:S(2)}) async-start(), calls=%async_computation.4 | async-start | bytes 1179648 | tf_op jit(solution)/shard_map/reduce_scatter | solution.py:122
  18.1 4.0 copy-start.35
  20.7 2.7 copy-start.2
  24.8 1.7 copy-start.3
  26.5 2.5 copy-start.21
  26.5 26.8 %copy-start.23 = (f32[768]{0:T(1024)S(1)}, f32[768]{0:T(1024)}, u32[]{:S(2)}) copy-start(f32[768]{0:T(1024)} %param.15) | copy-start | bytes 9220
  26.5 26.8 %copy-start.29 = (f32[768]{0:T(1024)S(1)}, f32[768]{0:T(1024)}, u32[]{:S(2)}) copy-start(f32[768]{0:T(1024)} %param.16) | copy-start | bytes 9220
  28.2 0.8 copy-start.10
  30.4 59.4 %reduce-scatter.7.cloned.1.call-start = ((), (), s32[]{:S(2)}) async-start(), calls=%async_computation.5 | async-start | bytes 1179648 | tf_op jit(solution)/shard_map/reduce_scatter | solution.py:132
  52.0 16.7 %copy-start.25 = (f32[256]{0:T(256)}, f32[256]{0:T(256)S(1)}, u32[]{:S(2)}) copy-start(f32[256]{0:T(256)S(1)} %broadcast_multiply_fusion.5) | copy-start | bytes 3076
  53.3 15.4 %copy-start.27 = (f32[256]{0:T(256)}, f32[256]{0:T(256)S(1)}, u32[]{:S(2)}) copy-start(f32[256]{0:T(256)S(1)} %add_rsqrt_fusion.1) | copy-start | bytes 3076
  65.9 2.8 copy-start.12
  65.9 4.0 copy-start.38
  68.7 1.2 copy-start.16
  69.9 20.0 %copy-start.5 = (bf16[256,768]{1,0:T(8,128)(2,1)S(1)}, bf16[256,768]{1,0:T(8,128)(2,1)}, u32[]{:S(2)}) copy-start(bf16[256,768]{1,0:T(8,128)(2,1)} %reduce-scatter.5.cloned.1.call-done) | copy-start | bytes 1179652
  72.2 65.1 %reduce-scatter.9.cloned.1.call-start = ((), (), s32[]{:S(2)}) async-start(), calls=%async_computation.6 | async-start | bytes 1179648 | tf_op jit(solution)/shard_map/reduce_scatter | solution.py:148
  89.9 3.9 copy-start.18
  89.9 3.9 copy-start.30
  89.9 3.9 copy-start.37
  91.3 15.3 %copy-start.39 = (bf16[1536,768]{1,0:T(8,128)(2,1)S(1)}, bf16[1536,768]{1,0:T(8,128)(2,1)}, u32[]{:S(2)}) copy-start(bf16[1536,768]{1,0:T(8,128)(2,1)} %param.18) | copy-start | bytes 7077892
  91.3 15.3 %copy-start.40 = (f32[512,1536]{1,0:T(8,128)S(1)}, f32[512,1536]{1,0:T(8,128)}, u32[]{:S(2)}) copy-start(f32[512,1536]{1,0:T(8,128)} %get-tuple-element.92) | copy-start | bytes 9437188
  106.7 2.4 copy-start.14
  109.1 1.1 copy-start.19
  112.5 485.1 %reduce-scatter.11.cloned.1.call-start = ((), (), s32[]{:S(2)}) async-start(), calls=%async_computation.7 | async-start | bytes 1179648 | tf_op jit(solution)/shard_map/reduce_scatter | solution.py:167
  122.1 5.8 copy-start.15
  122.1 5.8 copy-start.17
  131.5 5.8 copy-start.9
  131.5 5.8 copy-start.24
  131.5 5.8 copy-start.26
  131.5 5.8 copy-start.28
  137.4 14.9 %copy-start.22 = (bf16[384,768]{1,0:T(8,128)(2,1)S(1)}, bf16[384,768]{1,0:T(8,128)(2,1)}, u32[]{:S(2)}) copy-start(bf16[384,768]{1,0:T(8,128)(2,1)} %param.14) | copy-start | bytes 1769476
  139.5 13.3 %copy-start.7 = (bf16[512,1152]{0,1:T(8,128)(2,1)S(1)}, bf16[512,1152]{0,1:T(8,128)(2,1)}, u32[]{:S(2)}) copy-start(bf16[512,1152]{0,1:T(8,128)(2,1)} %copy.37) | copy-start | bytes 3538948
  139.5 13.3 %copy-start.36 = (pred[512]{0:T(512)(128)(4,1)S(1)}, pred[512]{0:T(512)(128)(4,1)}, u32[]{:S(2)}) copy-start(pred[512]{0:T(512)(128)(4,1)} %copy-done.35) | copy-start | bytes 1540
  152.8 4.6 slice-start
  152.8 4.7 slice-start.1
  159.7 1.9 copy-start.4
  160.3 2.3 copy-start.11
  163.3 2.9 copy-start.8
  182.0 1.2 copy-start.31
  182.0 1.2 copy-start.32
  182.0 1.2 copy-start.33
  182.0 1.2 copy-start.34
  277.4 465.9 %all-reduce.6.cloned.1.call-start = ((), (), s32[]{:S(2)}) async-start(), calls=%async_computation.8 | async-start | bytes 14168064
  586.9 1.0 copy-start.20
  586.9 10.8 %copy-start.13 = (f32[256,768]{1,0:T(8,128)S(1)}, f32[256,768]{1,0:T(8,128)}, u32[]{:S(2)}) copy-start(f32[256,768]{1,0:T(8,128)} %get-tuple-element.75) | copy-start | bytes 2359300
  775.0 8.0 %copy-start.1 = (bf16[768,1536]{1,0:T(8,128)(2,1)S(1)}, bf16[768,1536]{1,0:T(8,128)(2,1)}, u32[]{:S(2)}) copy-start(bf16[768,1536]{1,0:T(8,128)(2,1)} %param.17) | copy-start | bytes 7077892
Sparse Core Ops, SparseCore 0:
  30.5 20.2 reduce-scatter.4
  72.3 17.5 reduce-scatter.6
  112.7 17.4 reduce-scatter.8
  277.5 18.2 reduce-scatter.10
  587.0 156.2 all-reduce.5
where the time goes:
time: 798 us; the launch traced here: 790 us
  blocking collectives  358 us (45%)
  local copies, waits for them, and re-layouts  181 us (23%)
  waiting for transfers between devices  172 us (22%)
  matrix products  41.3 us (5%)
  other arithmetic  21.2 us (3%)
  between operations  16.2 us (2%)
    unnamed x1, blocking collectives  297 us
    unnamed x6, waiting for transfers between devices  134 us
    unnamed x101, local copies, waits for them, and re-layouts  124 us
    slice x7, local copies, waits for them, and re-layouts, on_device(): results.append(summed[start_at:start_at + extent].reshape(member.shape))  24.9 us
    reduce_scatter x1, waiting for transfers between devices, on_device(): lax.psum_scatter(jnp.dot(attended_rows, weight_out, preferred_element_typ...  20.3 us
    reduce_scatter x1, waiting for transfers between devices, on_device(): lax.psum_scatter(jnp.dot(activated, weight_down, preferred_element_type=j...  17.6 us
  transfers between devices with their start and end apart: 5, of which 3 were waited for; matrix products, arithmetic and copies ran while one was open for 5% of the time, Pallas kernels for 0%

commit v1 on v0

v1 whole, which is shorter than its diff:
```python
import functools

import jax
import jax.numpy as jnp
from jax import lax
from jax.experimental import pallas as pl
from jax.experimental.pallas import tpu as pltpu
from jax.sharding import PartitionSpec as P

HEAD_DIM = 64
EPSILON = 1e-05
MESH = pl.DeviceIdType.MESH
BF16 = jnp.bfloat16
F32 = jnp.float32
ANY = pl.BlockSpec(memory_space=pl.ANY)
VMEM_LIMIT = 63 * 2**20

CHUNK = 128
SUB = 384
SMALL = 64


def dot(left, right, left_dim, right_dim):
    return lax.dot_general(
        left, right, (((left_dim,), (right_dim,)), ((), ())), preferred_element_type=F32
    )


def row_mean(values):
    return jnp.sum(values, axis=-1, keepdims=True) * (1.0 / values.shape[-1])


def norm_forward(values):
    centred = values - row_mean(values)
    inverse = lax.rsqrt(row_mean(centred * centred) + EPSILON)
    return centred * inverse, inverse


def norm_backward(scaled, unit, inverse):
    return inverse * (scaled - row_mean(scaled) - unit * row_mean(scaled * unit))


class Layout:
    def __init__(self, width, qkv_cols, hidden):
        assert width == 2 * SUB and qkv_cols == SUB and hidden % SUB == 0
        self.subs = []
        start = 0
        for name, count, rows in (
            ("down", hidden // SUB, SUB),
            ("up", hidden // SUB, SUB),
            ("out", 1, SUB + SMALL),
            ("qkv", qkv_cols // 128, SUB),
        ):
            for index in range(count):
                self.subs.append((name, index, start, rows))
                start += rows
        self.rows = start


def layer_kernel(
    length_ref,
    tokens_hbm,
    wqkv_hbm,
    wout_hbm,
    gain_one_ref,
    bias_one_ref,
    wup_hbm,
    wdown_hbm,
    gain_two_ref,
    bias_two_ref,
    cot_hbm,
    out_hbm,
    grad_hbm,
    parts_hbm,
    tokens,
    cot,
    wqkv,
    wout,
    wup,
    wdown,
    packed,
    probs,
    attended,
    mine,
    theirs,
    unit_one,
    inv_one,
    normed,
    normed_low,
    slope,
    activated,
    grad_up_in,
    grad_res,
    grad_low,
    grad_att,
    grad_key,
    grad_val,
    grad_packed,
    small,
    parts,
    in_sem,
    out_sem,
    send_sem,
    recv_sem,
    *,
    layout,
):
    rows, width = tokens.shape
    hidden = wup.shape[1]
    cols = wout.shape[0]
    pairs = cols // 128
    chunks = rows // CHUNK
    scaling = HEAD_DIM**-0.5
    other = {"tp": 1 - lax.axis_index("tp")}

    barrier = pltpu.get_barrier_semaphore()
    pl.semaphore_signal(barrier, 1, device_id=other, device_id_type=MESH)

    loads = [
        pltpu.make_async_copy(source, target, in_sem.at[place])
        for place, (source, target) in enumerate(
            (
                (tokens_hbm, tokens),
                (wqkv_hbm, wqkv),
                (wout_hbm, wout),
                (wup_hbm, wup),
                (wdown_hbm, wdown),
                (cot_hbm, cot),
            )
        )
    ]
    for load in loads:
        load.start()

    def at(index):
        return pl.ds(pl.multiple_of(index * CHUNK, CHUNK), CHUNK)

    def exchange(which, index):
        return pltpu.make_async_remote_copy(
            src_ref=mine.at[which, at(index)],
            dst_ref=theirs.at[which, at(index)],
            send_sem=send_sem.at[which, index],
            recv_sem=recv_sem.at[which, index],
            device_id=other,
            device_id_type=MESH,
        )

    def received(which, index):
        place = at(index)
        return mine[which, place, :].astype(F32) + theirs[which, place, :].astype(F32)

    small[...] = jnp.zeros_like(small)
    grad_key[...] = jnp.zeros_like(grad_key)
    grad_val[...] = jnp.zeros_like(grad_val)

    lane = lax.broadcasted_iota(jnp.int32, (1, 128), 1)
    first = jnp.where(lane < HEAD_DIM, 1.0, 0.0).astype(BF16)
    second = jnp.where(lane < HEAD_DIM, 0.0, 1.0).astype(BF16)
    live = lax.broadcasted_iota(jnp.int32, (1, rows), 1) < length_ref[0]

    def stacked(block):
        return jnp.concatenate([block * first, block * second], axis=0)

    def merged(both):
        return jnp.where(lane < HEAD_DIM, both[:CHUNK], both[CHUNK:])

    loads[0].wait()
    loads[1].wait()

    def project(index, carry):
        place = at(index)
        for part in range(3):
            value = dot(tokens[place, :], wqkv[part], 1, 0).astype(BF16)
            packed[part, place, :] = value * BF16(scaling) if part == 0 else value
        return carry

    lax.fori_loop(0, chunks, project, 0)
    loads[2].wait()
    pl.semaphore_wait(barrier, 1)

    def attend(index, carry):
        place = at(index)
        for pair in range(pairs):
            span = slice(pair * 128, pair * 128 + 128)
            scores = dot(stacked(packed[0, place, span]), packed[1, :, span], 1, 1)
            scores = jnp.where(live, scores, -1000000000.0)
            expo = jnp.exp(scores - jnp.max(scores, axis=-1, keepdims=True))
            total = jnp.sum(expo, axis=-1, keepdims=True)
            low = (expo * (1.0 / total)).astype(BF16)
            probs[pair * chunks + index] = low
            attended[place, span] = merged(dot(low, packed[2, :, span], 1, 0)).astype(BF16)
        mine[0, place, :] = dot(attended[place, :], wout[...], 1, 0).astype(BF16)
        exchange(0, index).start()
        return carry

    lax.fori_loop(0, chunks, attend, 0)
    loads[3].wait()
    loads[4].wait()
    loads[5].wait()

    def feed(index, carry):
        place = at(index)
        exchange(0, index).wait()
        unit, inverse = norm_forward(tokens[place, :].astype(F32) + received(0, index))
        unit_one[place, :] = unit
        inv_one[place, :] = inverse
        value = unit * gain_one_ref[...] + bias_one_ref[...]
        normed[place, :] = value
        normed_low[place, :] = value.astype(BF16)
        for start in range(0, hidden, SUB):
            span = slice(start, start + SUB)
            upward = dot(normed_low[place, :], wup[:, span], 1, 0)
            share = 0.5 + 0.5 * lax.erf(upward * 0.7071067811865476)
            activated[place, span] = (upward * share).astype(BF16)
            slope[place, span] = share + upward * jnp.exp(upward * upward * -0.5) * 0.3989422804014327
        mine[1, place, :] = dot(activated[place, :], wdown[...], 1, 0).astype(BF16)
        exchange(1, index).start()
        return carry

    lax.fori_loop(0, chunks, feed, 0)

    def turn(index, carry):
        place = at(index)
        exchange(1, index).wait()
        unit, inverse = norm_forward(normed[place, :] + received(1, index))
        mine[2, place, :] = (unit * gain_two_ref[...] + bias_two_ref[...]).astype(BF16)
        pltpu.make_async_copy(mine.at[2, place], out_hbm.at[place], out_sem.at[0, index]).start()
        flow = cot[place, :].astype(F32)
        small[2:3, :] += jnp.sum(flow * unit, axis=0, keepdims=True)
        small[3:4, :] += jnp.sum(flow, axis=0, keepdims=True)
        grad = norm_backward(flow * gain_two_ref[...], unit, inverse)
        grad_res[place, :] = grad
        grad_low[0, place, :] = grad.astype(BF16)
        for start in range(0, hidden, SUB):
            span = slice(start, start + SUB)
            grad_act = dot(grad_low[0, place, :], wdown[span, :], 1, 1)
            grad_up_in[place, span] = (grad_act * slope[place, span]).astype(BF16)
        mine[3, place, :] = dot(grad_up_in[place, :], wup[...], 1, 1).astype(BF16)
        exchange(3, index).start()
        return carry

    lax.fori_loop(0, chunks, turn, 0)

    for name, which, start, extent in layout.subs:
        if name == "down":
            parts[start : start + extent, :] = dot(
                activated[:, which * SUB : which * SUB + SUB], grad_low[0], 0, 0
            ).astype(BF16)
        if name == "up":
            down_at, right_at = which % 2 * SUB, which // 2 * width
            parts[start : start + extent, :] = dot(
                normed_low[:, down_at : down_at + SUB],
                grad_up_in[:, right_at : right_at + width],
                0,
                0,
            ).astype(BF16)

    def attend_back(index, carry):
        place = at(index)
        exchange(3, index).wait()
        unit = unit_one[place, :]
        flow = grad_res[place, :] + received(3, index)
        small[0:1, :] += jnp.sum(flow * unit, axis=0, keepdims=True)
        small[1:2, :] += jnp.sum(flow, axis=0, keepdims=True)
        grad = norm_backward(flow * gain_one_ref[...], unit, inv_one[place, :])
        grad_res[place, :] = grad
        grad_low[1, place, :] = grad.astype(BF16)
        grad_att[place, :] = dot(grad_low[1, place, :], wout[...], 1, 1).astype(BF16)
        for pair in range(pairs):
            span = slice(pair * 128, pair * 128 + 128)
            low = probs[pair * chunks + index]
            pull = stacked(grad_att[place, span])
            seen = attended[place, span].astype(F32)
            centre = jnp.sum(
                pull.astype(F32) * jnp.concatenate([seen, seen], axis=0), axis=-1, keepdims=True
            )
            grad_probs = dot(pull, packed[2, :, span], 1, 1)
            grad_scores = (low.astype(F32) * (grad_probs - centre)).astype(BF16)
            grad_val[:, span] += dot(low, pull, 0, 0)
            grad_key[:, span] += dot(grad_scores, stacked(packed[0, place, span]), 0, 0)
            grad_query = merged(dot(grad_scores, packed[1, :, span], 1, 0)) * scaling
            grad_packed[0, place, span] = grad_query.astype(BF16)
        return carry

    lax.fori_loop(0, chunks, attend_back, 0)
    grad_packed[1] = grad_key[...].astype(BF16)
    grad_packed[2] = grad_val[...].astype(BF16)

    def leave(index, carry):
        place = at(index)
        total = dot(grad_packed[0, place, :], wqkv[0], 1, 1)
        total += dot(grad_packed[1, place, :], wqkv[1], 1, 1)
        total += dot(grad_packed[2, place, :], wqkv[2], 1, 1)
        mine[4, place, :] = total.astype(BF16)
        exchange(4, index).start()
        return carry

    lax.fori_loop(0, chunks, leave, 0)

    for name, which, start, extent in layout.subs:
        if name == "out":
            parts[start : start + SUB, :] = dot(attended[...], grad_low[1], 0, 0).astype(BF16)
            parts[start + SUB : start + extent, :] = small[...].astype(BF16)
        if name == "qkv":
            span = slice(which * 128, which * 128 + 128)
            for part in range(3):
                value = dot(tokens[...], grad_packed[part, :, span], 0, 0).astype(BF16)
                for half in range(2):
                    left = half * SUB + part * 128
                    parts[start : start + SUB, left : left + 128] = value[
                        half * SUB : half * SUB + SUB
                    ]

    flush = pltpu.make_async_copy(parts, parts_hbm, in_sem.at[6])
    flush.start()

    def finish(index, carry):
        place = at(index)
        exchange(4, index).wait()
        mine[5, place, :] = (grad_res[place, :] + received(4, index)).astype(BF16)
        pltpu.make_async_copy(mine.at[5, place], grad_hbm.at[place], out_sem.at[1, index]).start()
        return carry

    lax.fori_loop(0, chunks, finish, 0)

    def drain(index, carry):
        place = at(index)
        pltpu.make_async_copy(mine.at[2, place], out_hbm.at[place], out_sem.at[0, index]).wait()
        pltpu.make_async_copy(mine.at[5, place], grad_hbm.at[place], out_sem.at[1, index]).wait()
        return carry

    lax.fori_loop(0, chunks, drain, 0)
    flush.wait()


class Sum:
    def __init__(self, layout, parts, totals, near, across, inflow, middle, send_sem, recv_sem):
        self.layout, self.parts, self.totals = layout, parts, totals
        self.near, self.across, self.inflow, self.middle = near, across, inflow, middle
        self.send_sem, self.recv_sem = send_sem, recv_sem
        line, group = lax.axis_size("dp"), lax.axis_size("dq")
        assert group == 4 and line % 2 == 0
        self.spot, place = lax.axis_index("dp"), lax.axis_index("dq")
        self.core, self.chip = lax.rem(place, 2), lax.div(place, 2)
        self.even, self.odd = self.core == 0, self.core == 1
        lower = self.spot < line // 2
        self.side = jnp.where(lower, 0, 1)
        self.centre = jnp.logical_or(self.spot == line // 2 - 1, self.spot == line // 2)
        self.outer = jnp.logical_and(self.spot > 0, self.spot < line - 1)
        if line == 2:
            self.outer = self.spot < 0
        self.to_core = {"dq": place + 1 - 2 * self.core}
        self.to_chip = {"dq": lax.rem(place + 2, 4)}
        self.inward = {"dp": jnp.where(lower, self.spot + 1, self.spot - 1)}
        self.outward = {"dp": jnp.where(lower, self.spot - 1, self.spot + 1)}

    def greet(self, barrier):
        for device in (self.to_core, self.to_chip, self.inward):
            pl.semaphore_signal(barrier, 1, device_id=device, device_id_type=MESH)

        @pl.when(self.outer)
        def _():
            pl.semaphore_signal(barrier, 1, device_id=self.outward, device_id_type=MESH)

    def meet(self, barrier, more=0):
        pl.semaphore_wait(barrier, 3 + more + jnp.where(self.outer, 1, 0))

    def span(self, k, core=None, chip=None):
        _, _, start, rows = self.layout.subs[k]
        if core is None:
            return pl.ds(start, rows)
        first = start + core * (rows // 2)
        if chip is None:
            return pl.ds(pl.multiple_of(first, 16), rows // 2)
        return pl.ds(pl.multiple_of(first + chip * (rows // 4), 16), rows // 4)

    def slot(self, k, share):
        _, _, start, rows = self.layout.subs[k]
        return pl.ds(start // share, rows // share)

    def copy(self, kind, k, source, target, device):
        return pltpu.make_async_remote_copy(
            src_ref=source,
            dst_ref=target,
            send_sem=self.send_sem.at[kind, k],
            recv_sem=self.recv_sem.at[kind, k],
            device_id=device,
            device_id_type=MESH,
        )

    def add(self, place, arrived, target=None):
        value = self.parts[place, :].astype(F32) + arrived.astype(F32)
        target = self.parts if target is None else target
        target[place, :] = value.astype(BF16)

    def half(self, k):
        return self.span(k, self.core)

    def quarter(self, k, which):
        return self.span(k, self.core, which)

    def over_core(self, k):
        return self.copy(
            0, k, self.parts.at[self.span(k, 1 - self.core)], self.near.at[self.slot(k, 2)], self.to_core
        )

    def over_chip(self, k, which):
        return self.copy(
            1, k, self.parts.at[self.quarter(k, which)], self.across.at[self.slot(k, 4)], self.to_chip
        )

    def run_in(self, k, place, share):
        return self.copy(2, k, self.parts.at[place], self.inflow.at[self.slot(k, share)], self.inward)

    def swap(self, k, which):
        return self.copy(
            3, k, self.parts.at[self.quarter(k, which)], self.middle.at[self.slot(k, 4)], self.inward
        )

    def hand_on(self, kind, k, place, device):
        return self.copy(kind, k, self.totals.at[place], self.totals.at[place], device)

    def pass_even(self, k):
        mine = self.quarter(k, self.chip)

        @pl.when(self.centre)
        def _():
            self.swap(k, self.chip).start()

        @pl.when(jnp.logical_not(self.centre))
        def _():
            self.run_in(k, mine, 4).start()

    def pass_odd(self, k):
        @pl.when(self.centre)
        def _():
            self.swap(k, 1 - self.side).start()

        @pl.when(jnp.logical_not(self.centre))
        def _():
            self.run_in(k, self.half(k), 2).start()

    def stage(self, number, k):
        even, odd, centre, outer = self.even, self.odd, self.centre, self.outer
        both = jnp.logical_and
        inner = jnp.logical_not(centre)
        mine = self.quarter(k, self.chip)
        half = self.half(k)

        def when(*conditions):
            return pl.when(functools.reduce(both, conditions))

        if number == 0:
            self.over_core(k).start()
        if number == 1:
            self.over_core(k).wait()
            self.add(half, self.near[self.slot(k, 2), :])

            @when(even)
            def _():
                self.over_chip(k, 1 - self.chip).start()

            @when(odd, jnp.logical_not(outer))
            def _():
                self.pass_odd(k)

        if number == 2:

            @when(even)
            def _():
                self.over_chip(k, 1 - self.chip).wait()
                self.add(mine, self.across[self.slot(k, 4), :])

            @when(even, jnp.logical_not(outer))
            def _():
                self.pass_even(k)

            @when(odd, outer)
            def _():
                self.run_in(k, half, 2).wait_recv()
                self.add(half, self.inflow[self.slot(k, 2), :])
                self.pass_odd(k)

        if number == 3:

            @when(even, outer)
            def _():
                self.run_in(k, mine, 4).wait_recv()
                self.add(mine, self.inflow[self.slot(k, 4), :])
                self.pass_even(k)

            @when(odd, centre)
            def _():
                self.swap(k, 1 - self.side).wait()
                self.add(self.quarter(k, self.side), self.middle[self.slot(k, 4), :])
                self.over_chip(k, self.side).start()

        if number == 4:

            @when(even, centre)
            def _():
                self.swap(k, self.chip).wait()
                self.add(mine, self.middle[self.slot(k, 4), :], self.totals)

            @when(even, centre, outer)
            def _():
                self.hand_on(4, k, mine, self.outward).start()

            @when(even, centre)
            def _():
                self.hand_on(5, k, mine, self.to_chip).start()

            @when(odd, centre)
            def _():
                self.over_chip(k, self.side).wait()
                self.add(self.quarter(k, self.side), self.across[self.slot(k, 4), :], self.totals)
                self.hand_on(5, k, self.quarter(k, self.side), self.inward).start()

        if number == 5:

            @when(even, inner)
            def _():
                self.run_in(k, mine, 4).wait_send()
                self.hand_on(4, k, mine, self.inward).wait_recv()

            @when(even, inner, outer)
            def _():
                self.hand_on(4, k, mine, self.outward).start()

            @when(even, inner)
            def _():
                self.hand_on(5, k, mine, self.to_chip).start()

            @when(odd, centre)
            def _():
                self.hand_on(5, k, self.quarter(k, self.side), self.inward).wait_send()
                self.hand_on(5, k, self.quarter(k, 1 - self.side), self.inward).wait_recv()

            @when(odd, centre, outer)
            def _():
                self.hand_on(4, k, half, self.outward).start()

            @when(odd, centre)
            def _():
                self.hand_on(6, k, half, self.to_core).start()

        if number == 6:

            @when(even)
            def _():
                self.hand_on(5, k, mine, self.to_chip).wait_send()
                self.hand_on(5, k, self.quarter(k, 1 - self.chip), self.to_chip).wait_recv()
                self.hand_on(6, k, half, self.to_core).start()

            @when(odd, inner)
            def _():
                self.run_in(k, half, 2).wait_send()
                self.hand_on(4, k, half, self.inward).wait_recv()

            @when(odd, inner, outer)
            def _():
                self.hand_on(4, k, half, self.outward).start()

            @when(odd, inner)
            def _():
                self.hand_on(6, k, half, self.to_core).start()

        if number == 7:

            @when(even, outer)
            def _():
                self.hand_on(4, k, mine, self.outward).wait_send()

            @when(odd, outer)
            def _():
                self.hand_on(4, k, half, self.outward).wait_send()

            self.hand_on(6, k, half, self.to_core).wait_send()
            self.hand_on(6, k, self.span(k, 1 - self.core), self.to_core).wait_recv()


STAGES = 8


def sum_kernel(
    parts_hbm, sums_hbm, parts, totals, near, across, inflow, middle, in_sem, out_sem, send_sem, recv_sem, *, layout
):
    total = Sum(layout, parts, totals, near, across, inflow, middle, send_sem, recv_sem)
    barrier = pltpu.get_barrier_semaphore()
    total.greet(barrier)
    count = len(layout.subs)

    def load(k):
        return pltpu.make_async_copy(
            parts_hbm.at[total.span(k)], parts.at[total.span(k)], in_sem.at[k]
        )

    def store(k):
        return pltpu.make_async_copy(
            totals.at[total.span(k)], sums_hbm.at[total.span(k)], out_sem.at[k]
        )

    for k in range(count):
        load(k).start()
    total.meet(barrier)
    for step in range(count + STAGES - 1):
        for number in reversed(range(STAGES)):
            k = step - number
            if 0 <= k < count:
                if number == 0:
                    load(k).wait()
                total.stage(number, k)
                if number == STAGES - 1:
                    store(k).start()
    for k in range(count):
        store(k).wait()


def widen_kernel(
    sums_hbm,
    out_in,
    grad_in,
    out_hbm,
    grad_hbm,
    qkv_hbm,
    wout_hbm,
    gain_one_hbm,
    bias_one_hbm,
    up_hbm,
    down_hbm,
    gain_two_hbm,
    bias_two_hbm,
    sums,
    wide,
    rows_in,
    in_sem,
    out_sem,
    row_sem,
    *,
    layout,
):
    slots = wide.shape[0]
    width = sums.shape[1]

    def load(k):
        _, _, start, rows = layout.subs[k]
        return pltpu.make_async_copy(
            sums_hbm.at[pl.ds(start, rows)], sums.at[pl.ds(start, rows)], in_sem.at[k]
        )

    def stores(k):
        name, which, _, _ = layout.subs[k]
        slot = k % slots
        block = wide.at[slot, pl.ds(0, SUB)]
        if name == "down":
            pieces = [(block, down_hbm.at[pl.ds(which * SUB, SUB)])]
        elif name == "up":
            pieces = [
                (block, up_hbm.at[pl.ds(which % 2 * SUB, SUB), pl.ds(which // 2 * width, width)])
            ]
        elif name == "out":
            pieces = [(block, wout_hbm)]
            for row, target in enumerate((gain_one_hbm, bias_one_hbm, gain_two_hbm, bias_two_hbm)):
                pieces.append((wide.at[slot, pl.ds(SUB + 8 * row, 1)], target))
        else:
            pieces = [
                (
                    wide.at[slot, pl.ds(0, SUB), pl.ds(half * SUB + part * 128, 128)],
                    qkv_hbm.at[part, pl.ds(half * SUB, SUB), pl.ds(which * 128, 128)],
                )
                for half in range(2)
                for part in range(3)
            ]
        return [
            pltpu.make_async_copy(source, target, out_sem.at[slot, place])
            for place, (source, target) in enumerate(pieces)
        ]

    through = ((out_in, out_hbm), (grad_in, grad_hbm))
    for place, (source, _) in enumerate(through):
        pltpu.make_async_copy(source, rows_in.at[place], row_sem.at[place]).start()
    for k in range(len(layout.subs)):
        load(k).start()
    for place, (source, target) in enumerate(through):
        pltpu.make_async_copy(source, rows_in.at[place], row_sem.at[place]).wait()
        pltpu.make_async_copy(rows_in.at[place], target, row_sem.at[2 + place]).start()
    for k, (name, _, start, _) in enumerate(layout.subs):
        load(k).wait()
        if k >= slots:
            for store in stores(k - slots):
                store.wait()
        wide[k % slots, 0:SUB, :] = sums[start : start + SUB, :].astype(F32)
        if name == "out":
            low = sums[start + SUB : start + SUB + 16, :].astype(F32)
            for row in range(4):
                wide[k % slots, SUB + 8 * row : SUB + 8 * row + 1, :] = low[row : row + 1]
        for store in stores(k):
            store.start()
    for k in range(len(layout.subs) - slots, len(layout.subs)):
        for store in stores(k):
            store.wait()
    for place, (_, target) in enumerate(through):
        pltpu.make_async_copy(rows_in.at[place], target, row_sem.at[2 + place]).wait()


def on_device(
    tokens,
    lengths,
    weight_qkv,
    weight_out,
    gain_one,
    bias_one,
    weight_up,
    weight_down,
    gain_two,
    bias_two,
    cotangent,
):
    seq_count, rows, width = tokens.shape
    cols, hidden = weight_out.shape[0], weight_up.shape[1]
    assert seq_count == 1 and rows % CHUNK == 0 and lax.axis_size("tp") == 2
    layout = Layout(width, cols, hidden)
    count = len(layout.subs)
    chunks = rows // CHUNK
    pairs = cols // 128
    whole = pl.BlockSpec(memory_space=pltpu.VMEM)
    out_rows, grad_rows, parts = pl.pallas_call(
        functools.partial(layer_kernel, layout=layout),
        name="layer",
        out_shape=(
            jax.ShapeDtypeStruct((rows, width), BF16),
            jax.ShapeDtypeStruct((rows, width), BF16),
            jax.ShapeDtypeStruct((layout.rows, width), BF16),
        ),
        in_specs=[
            pl.BlockSpec(memory_space=pltpu.SMEM),
            ANY,
            ANY,
            ANY,
            whole,
            whole,
            ANY,
            ANY,
            whole,
            whole,
            ANY,
        ],
        out_specs=(ANY, ANY, ANY),
        scratch_shapes=[
            pltpu.VMEM((rows, width), BF16),
            pltpu.VMEM((rows, width), BF16),
            pltpu.VMEM((3, width, cols), BF16),
            pltpu.VMEM((cols, width), BF16),
            pltpu.VMEM((width, hidden), BF16),
            pltpu.VMEM((hidden, width), BF16),
            pltpu.VMEM((3, rows, cols), BF16),
            pltpu.VMEM((pairs * chunks, 2 * CHUNK, rows), BF16),
            pltpu.VMEM((rows, cols), BF16),
            pltpu.VMEM((6, rows, width), BF16),
            pltpu.VMEM((5, rows, width), BF16),
            pltpu.VMEM((rows, width), F32),
            pltpu.VMEM((rows, 1), F32),
            pltpu.VMEM((rows, width), F32),
            pltpu.VMEM((rows, width), BF16),
            pltpu.VMEM((rows, hidden), F32),
            pltpu.VMEM((rows, hidden), BF16),
            pltpu.VMEM((rows, hidden), BF16),
            pltpu.VMEM((rows, width), F32),
            pltpu.VMEM((2, rows, width), BF16),
            pltpu.VMEM((rows, cols), BF16),
            pltpu.VMEM((rows, cols), F32),
            pltpu.VMEM((rows, cols), F32),
            pltpu.VMEM((3, rows, cols), BF16),
            pltpu.VMEM((SMALL, width), F32),
            pltpu.VMEM((layout.rows, width), BF16),
            pltpu.SemaphoreType.DMA((7,)),
            pltpu.SemaphoreType.DMA((2, chunks)),
            pltpu.SemaphoreType.DMA((5, chunks)),
            pltpu.SemaphoreType.DMA((5, chunks)),
        ],
        compiler_params=pltpu.CompilerParams(
            collective_id=1, has_side_effects=True, vmem_limit_bytes=VMEM_LIMIT
        ),
    )(
        lengths,
        tokens.reshape(rows, width),
        jnp.transpose(weight_qkv, (1, 0, 2)),
        weight_out,
        gain_one.reshape(1, width),
        bias_one.reshape(1, width),
        weight_up,
        weight_down,
        gain_two.reshape(1, width),
        bias_two.reshape(1, width),
        cotangent.reshape(rows, width),
    )
    sums = pl.pallas_call(
        functools.partial(sum_kernel, layout=layout),
        name="sum",
        out_shape=jax.ShapeDtypeStruct((layout.rows, width), BF16),
        in_specs=[ANY],
        out_specs=ANY,
        scratch_shapes=[
            pltpu.VMEM((layout.rows, width), BF16),
            pltpu.VMEM((layout.rows, width), BF16),
            pltpu.VMEM((layout.rows // 2, width), BF16),
            pltpu.VMEM((layout.rows // 4, width), BF16),
            pltpu.VMEM((layout.rows // 2, width), BF16),
            pltpu.VMEM((layout.rows // 4, width), BF16),
            pltpu.SemaphoreType.DMA((count,)),
            pltpu.SemaphoreType.DMA((count,)),
            pltpu.SemaphoreType.DMA((7, count)),
            pltpu.SemaphoreType.DMA((7, count)),
        ],
        compiler_params=pltpu.CompilerParams(
            collective_id=2, has_side_effects=True, vmem_limit_bytes=VMEM_LIMIT
        ),
    )(parts)
    vector = jax.ShapeDtypeStruct((1, width), F32)
    results = pl.pallas_call(
        functools.partial(widen_kernel, layout=layout),
        name="widen",
        out_shape=(
            jax.ShapeDtypeStruct((rows, width), BF16),
            jax.ShapeDtypeStruct((rows, width), BF16),
            jax.ShapeDtypeStruct((3, width, cols), F32),
            jax.ShapeDtypeStruct((cols, width), F32),
            vector,
            vector,
            jax.ShapeDtypeStruct((width, hidden), F32),
            jax.ShapeDtypeStruct((hidden, width), F32),
            vector,
            vector,
        ),
        in_specs=[ANY] * 3,
        out_specs=(ANY,) * 10,
        scratch_shapes=[
            pltpu.VMEM((layout.rows, width), BF16),
            pltpu.VMEM((4, SUB + 32, width), F32),
            pltpu.VMEM((2, rows, width), BF16),
            pltpu.SemaphoreType.DMA((count,)),
            pltpu.SemaphoreType.DMA((4, 6)),
            pltpu.SemaphoreType.DMA((4,)),
        ],
        compiler_params=pltpu.CompilerParams(vmem_limit_bytes=VMEM_LIMIT),
    )(sums, out_rows, grad_rows)
    return (
        results[0].reshape(seq_count, rows, width),
        results[1].reshape(seq_count, rows, width),
        jnp.transpose(results[2], (1, 0, 2)),
        results[3],
        results[4].reshape(width),
        results[5].reshape(width),
        results[6],
        results[7],
        results[8].reshape(width),
        results[9].reshape(width),
    )


def solution(mesh):
    batch = P(("dp", "dq"), None, None)
    return jax.shard_map(
        on_device,
        mesh=mesh,
        in_specs=(
            batch,
            P(("dp", "dq")),
            P(None, None, "tp"),
            P("tp", None),
            P(),
            P(),
            P(None, "tp"),
            P("tp", None),
            P(),
            P(),
            batch,
        ),
        out_specs=(
            batch,
            batch,
            P(None, None, "tp"),
            P("tp", None),
            P(),
            P(),
            P(None, "tp"),
            P("tp", None),
            P(),
            P(),
        ),
        check_vma=False,
    )
```

time: 798 us -> 195 us (0.24)
  blocking collectives: 358 us -> 0 us
  Pallas kernels: 0 us -> 182 us
  local copies, waits for them, and re-layouts: 181 us -> 5.07 us
  waiting for transfers between devices: 172 us -> 0 us
  matrix products: 41.3 us -> 0 us
  other arithmetic: 21.2 us -> 5.14 us
  between operations: 16.2 us -> 1.32 us
    unnamed x1 -> x0, blocking collectives: 297 us -> none
    pallas_call x0 -> x3, Pallas kernels: none -> 182 us  [the longest x1 92.1 us: on_device(): pl.pallas_call(functools.partial(sum_kernel, layout=layout), name='sum',...]
    unnamed x6 -> x0, waiting for transfers between devices: 134 us -> none
    unnamed x101 -> x0, local copies, waits for them, and re-layouts: 124 us -> none
    all_gather x5 -> x0, blocking collectives: 53.9 us -> none  [the longest x1 11.5 us: on_device(): lax.all_gather(grad_res_two.astype(jnp.bfloat16), 'tp', axis=0, tiled=True)]
    dot_general x18 -> x0, matrix products: 41.3 us -> none  [the longest x4 12.2 us: contract_rows(): lax.dot_general(left, right, (((0,), (0,)), ((), ())), preferred_element_...]
    reduce_scatter x4 -> x0, waiting for transfers between devices: 37.9 us -> none  [the longest x1 20.3 us: on_device(): lax.psum_scatter(jnp.dot(attended_rows, weight_out, preferred_element_typ...]
    slice x7 -> x0, local copies, waits for them, and re-layouts: 24.9 us -> none  [on_device(): results.append(summed[start_at:start_at + extent].reshape(member.shape))]
  transfers between devices with their start and end apart: 5 -> 0, of which waited for: 3 -> 0; matrix products, arithmetic and copies ran while one was open for 5% -> 0% of each run, Pallas kernels for 0% -> 0%
where the time goes in v1:
time: 195 us; the launch traced here: 194 us
  Pallas kernels  182 us (93%)
  other arithmetic  5.14 us (3%)
  local copies, waits for them, and re-layouts  5.07 us (3%)
    pallas_call x1, Pallas kernels, on_device(): pl.pallas_call(functools.partial(sum_kernel, layout=layout), name='sum',...  92.1 us
    pallas_call x1, Pallas kernels, on_device(): pl.pallas_call(functools.partial(layer_kernel, layout=layout), name='laye...  81.3 us
    pallas_call x1, Pallas kernels, on_device(): pl.pallas_call(functools.partial(widen_kernel, layout=layout), name='wide...  8.93 us
    pallas_call x4, other arithmetic, on_device(): pl.pallas_call(functools.partial(widen_kernel, layout=layout), name='wide...  5.14 us

profile of v1, /device:TPU:0, one launch (start us, length us, event | category | flops | bytes accessed | tf_op | source)
XLA Modules:
  0.0 193.9 jit_solution(12440563070091147830)
XLA Ops:
  1.3 1.3 reshape.57.gain_one_ref
  2.6 1.3 reshape.58.bias_one_ref
  3.8 1.3 reshape.59.gain_two_ref
  5.1 1.3 reshape.60.bias_two_ref
  6.4 81.3 %layer.1 = (bf16[512,768]{1,0:T(8,128)(2,1)}, bf16[512,768]{1,0:T(8,128)(2,1)}, bf16[4672,768]{1,0:T(8,128)(2,1)}) custom-call(s32[1]{0:T(128)S(6)} %copy.21.length_ref, bf16[512,768]{1,0:T(8,128)(2,1)} %bitcast.7, bf16[3,768,384]{2,1,0:T(8,128)(2,1)} %bitcast.6, bf16[384,768]{1,0:T(8,128)(2,1)} %wout_hbm.1, f32[1,768]{1,0:T(1,128)} %reshape.57.gain_one_ref, ...), custom_call_target="tpu_custom_call" | custom-call | tf_op jit(solution)/shard_map/layer/pallas_call | solution.py:727
  87.7 92.1 %sum.1.sums_hbm = bf16[4672,768]{1,0:T(8,128)(2,1)} custom-call(bf16[4672,768]{1,0:T(8,128)(2,1)} %get-tuple-element.23.parts_hbm), custom_call_target="tpu_custom_call" | custom-call | tf_op jit(solution)/shard_map/sum/pallas_call | solution.py:797
  179.8 8.9 %widen.1 = (bf16[512,768]{1,0:T(8,128)(2,1)}, bf16[512,768]{1,0:T(8,128)(2,1)}, f32[3,768,384]{2,1,0:T(8,128)}, f32[384,768]{1,0:T(8,128)}, f32[1,768]{1,0:T(1,1...) custom-call(bf16[4672,768]{1,0:T(8,128)(2,1)} %sum.1.sums_hbm, ...), custom_call_target="tpu_custom_call" | custom-call | tf_op jit(solution)/shard_map/widen/pallas_call | solution.py:820
  188.8 1.3 reduce
  190.1 1.3 reduce.1
  191.4 1.3 reduce.2
  192.6 1.3 reduce.3

commit v2 on v1

v2 whole, which is shorter than its diff:
```python
import functools

import jax
import jax.numpy as jnp
from jax import lax
from jax.experimental import pallas as pl
from jax.experimental.pallas import tpu as pltpu
from jax.sharding import PartitionSpec as P

HEAD_DIM = 64
EPSILON = 1e-05
MESH = pl.DeviceIdType.MESH
BF16 = jnp.bfloat16
F32 = jnp.float32
ANY = pl.BlockSpec(memory_space=pl.ANY)
VMEM_LIMIT = 63 * 2**20

CHUNK = 128
SUB = 384
SMALL = 64


def dot(left, right, left_dim, right_dim):
    return lax.dot_general(
        left, right, (((left_dim,), (right_dim,)), ((), ())), preferred_element_type=F32
    )


def row_mean(values):
    return jnp.sum(values, axis=-1, keepdims=True) * (1.0 / values.shape[-1])


def norm_forward(values):
    centred = values - row_mean(values)
    inverse = lax.rsqrt(row_mean(centred * centred) + EPSILON)
    return centred * inverse, inverse


def norm_backward(scaled, unit, inverse):
    return inverse * (scaled - row_mean(scaled) - unit * row_mean(scaled * unit))


class Layout:
    def __init__(self, width, qkv_cols, hidden):
        assert width == 2 * SUB and qkv_cols == SUB and hidden % SUB == 0
        self.subs = []
        start = 0
        for name, count, rows in (
            ("down", hidden // SUB, SUB),
            ("up", hidden // SUB, SUB),
            ("out", 1, SUB + SMALL),
            ("qkv", qkv_cols // 128, SUB),
        ):
            for index in range(count):
                self.subs.append((name, index, start, rows))
                start += rows
        self.rows = start


class Sum:
    def __init__(self, layout, parts, totals, near, across, inflow, middle, send_sem, recv_sem):
        self.layout, self.parts, self.totals = layout, parts, totals
        self.near, self.across, self.inflow, self.middle = near, across, inflow, middle
        self.send_sem, self.recv_sem = send_sem, recv_sem
        line, group = lax.axis_size("dp"), lax.axis_size("dq")
        assert group == 4 and line % 2 == 0
        self.spot, place = lax.axis_index("dp"), lax.axis_index("dq")
        self.core, self.chip = lax.rem(place, 2), lax.div(place, 2)
        self.even, self.odd = self.core == 0, self.core == 1
        lower = self.spot < line // 2
        self.side = jnp.where(lower, 0, 1)
        self.centre = jnp.logical_or(self.spot == line // 2 - 1, self.spot == line // 2)
        self.inner = jnp.logical_not(self.centre)
        self.outer = jnp.logical_and(self.spot > 0, self.spot < line - 1)
        self.end = jnp.logical_not(self.outer)
        self.to_core = {"dq": place + 1 - 2 * self.core}
        self.to_chip = {"dq": lax.rem(place + 2, 4)}
        self.inward = {"dp": jnp.where(lower, self.spot + 1, self.spot - 1)}
        self.outward = {"dp": jnp.where(lower, self.spot - 1, self.spot + 1)}

    def greet(self, barrier):
        for device in (self.to_core, self.to_chip, self.inward):
            pl.semaphore_signal(barrier, 1, device_id=device, device_id_type=MESH)

        @pl.when(self.outer)
        def _():
            pl.semaphore_signal(barrier, 1, device_id=self.outward, device_id_type=MESH)

    def meet(self, barrier, more=0):
        pl.semaphore_wait(barrier, 3 + more + jnp.where(self.outer, 1, 0))

    def half(self, k, core=None):
        _, _, start, rows = self.layout.subs[k]
        first = start + (self.core if core is None else core) * (rows // 2)
        return pl.ds(pl.multiple_of(first, 16), rows // 2)

    def quarter(self, k, which):
        _, _, start, rows = self.layout.subs[k]
        first = start + self.core * (rows // 2) + which * (rows // 4)
        return pl.ds(pl.multiple_of(first, 16), rows // 4)

    def slot(self, k, share):
        _, _, start, rows = self.layout.subs[k]
        return pl.ds(start // share, rows // share)

    def copy(self, sent, arrived, k, source, target, device):
        return pltpu.make_async_remote_copy(
            src_ref=source,
            dst_ref=target,
            send_sem=self.send_sem.at[sent, k],
            recv_sem=self.recv_sem.at[arrived, k],
            device_id=device,
            device_id_type=MESH,
        )

    def add(self, k, place, buffer, share, target=None):
        arrived = buffer[self.slot(k, share), :]
        value = self.parts[place, :].astype(F32) + arrived.astype(F32)
        target = self.parts if target is None else target
        target[place, :] = value.astype(BF16)

    def over_core(self, k):
        near = self.near.at[self.slot(k, 2)]
        return self.copy(0, 0, k, self.parts.at[self.half(k, 1 - self.core)], near, self.to_core)

    def over_chip(self, k, which):
        across = self.across.at[self.slot(k, 4)]
        return self.copy(1, 1, k, self.parts.at[self.quarter(k, which)], across, self.to_chip)

    def run_in(self, k, which):
        inflow = self.inflow.at[self.slot(k, 4)]
        return self.copy(2, 2, k, self.parts.at[self.quarter(k, which)], inflow, self.inward)

    def swap(self, k, which):
        middle = self.middle.at[self.slot(k, 4)]
        return self.copy(3, 3, k, self.parts.at[self.quarter(k, which)], middle, self.inward)

    def run_out(self, k, which):
        middle = self.middle.at[self.slot(k, 4)]
        return self.copy(4, 3, k, self.parts.at[self.quarter(k, which)], middle, self.outward)

    def hand_on(self, sent, arrived, k, place, device):
        total = self.totals.at[place]
        return self.copy(sent, arrived, k, total, total, device)

    def send_in(self, k, which):
        @pl.when(self.centre)
        def _():
            self.swap(k, which).start()

        @pl.when(self.inner)
        def _():
            self.run_in(k, which).start()

    def total_in(self, k, which):
        place = self.quarter(k, which)

        @pl.when(self.centre)
        def _():
            self.hand_on(5, 6, k, place, self.inward).start()

        @pl.when(self.inner)
        def _():
            self.hand_on(5, 5, k, place, self.inward).start()

    def stage(self, number, k):
        even, odd, centre, inner, outer, end = (
            self.even,
            self.odd,
            self.centre,
            self.inner,
            self.outer,
            self.end,
        )
        own, rest = self.chip, 1 - self.chip
        to_out, to_in = self.side, 1 - self.side
        mine, half = self.quarter(k, own), self.half(k)

        def when(*conditions):
            return pl.when(functools.reduce(jnp.logical_and, conditions))

        if number == 0:
            self.over_core(k).start()
        if number == 1:
            self.over_core(k).wait_recv()
            self.add(k, half, self.near, 2)

            @when(even)
            def _():
                self.over_chip(k, rest).start()

            @when(odd, end)
            def _():
                self.send_in(k, to_in)

        if number == 2:

            @when(even)
            def _():
                self.over_chip(k, rest).wait_recv()
                self.add(k, mine, self.across, 4)

            @when(even, end)
            def _():
                self.send_in(k, own)

            @when(odd, outer)
            def _():
                self.run_in(k, to_in).wait_recv()
                self.add(k, self.quarter(k, to_in), self.inflow, 4)
                self.send_in(k, to_in)

        if number == 3:

            @when(even, outer)
            def _():
                self.run_in(k, own).wait_recv()
                self.add(k, mine, self.inflow, 4)
                self.send_in(k, own)

            @when(odd, outer)
            def _():
                self.swap(k, to_out).wait_recv()
                self.add(k, self.quarter(k, to_out), self.middle, 4)
                self.run_out(k, to_out).start()

        if number == 4:

            @when(even, centre)
            def _():
                self.swap(k, own).wait_recv()
                self.add(k, mine, self.middle, 4, self.totals)
                self.hand_on(5, 5, k, mine, self.to_chip).start()

            @when(even, centre, outer)
            def _():
                self.hand_on(4, 4, k, mine, self.outward).start()

            @when(odd, end)
            def _():
                self.swap(k, to_out).wait_recv()
                self.add(k, self.quarter(k, to_out), self.middle, 4)
                self.over_chip(k, to_out).start()

        if number == 5:

            @when(even, inner)
            def _():
                self.hand_on(4, 4, k, mine, self.inward).wait_recv()
                self.hand_on(5, 5, k, mine, self.to_chip).start()

            @when(even, inner, outer)
            def _():
                self.hand_on(4, 4, k, mine, self.outward).start()

            @when(odd, end)
            def _():
                self.over_chip(k, to_out).wait_recv()
                self.add(k, self.quarter(k, to_out), self.across, 4, self.totals)
                self.total_in(k, to_out)

        if number == 6:

            @when(even)
            def _():
                self.hand_on(5, 5, k, self.quarter(k, rest), self.to_chip).wait_recv()
                self.hand_on(7, 7, k, half, self.to_core).start()

            @when(odd, outer)
            def _():
                self.hand_on(5, 5, k, self.quarter(k, to_out), self.inward).wait_recv()
                self.total_in(k, to_out)

        if number == 7:

            @when(odd, outer)
            def _():
                self.hand_on(6, 6, k, self.quarter(k, to_in), self.outward).wait_recv()
                self.hand_on(6, 6, k, self.quarter(k, to_in), self.outward).start()
                self.hand_on(7, 7, k, half, self.to_core).start()

        if number == 8:

            @when(odd, end)
            def _():
                self.hand_on(6, 6, k, self.quarter(k, to_in), self.inward).wait_recv()
                self.hand_on(7, 7, k, half, self.to_core).start()

        if number == 9:
            self.hand_on(7, 7, k, self.half(k, 1 - self.core), self.to_core).wait_recv()

    def settle(self, k):
        own, mine = self.quarter(k, self.chip), self.quarter(k, self.chip)
        self.over_core(k).wait_send()
        self.hand_on(7, 7, k, self.half(k), self.to_core).wait_send()

        def when(*conditions):
            return pl.when(functools.reduce(jnp.logical_and, conditions))

        @when(self.even)
        def _():
            self.over_chip(k, 1 - self.chip).wait_send()
            self.hand_on(5, 5, k, mine, self.to_chip).wait_send()

        @when(self.even, self.outer)
        def _():
            self.hand_on(4, 4, k, mine, self.outward).wait_send()

        @when(self.centre)
        def _():
            self.swap(k, 0).wait_send()

        @when(self.inner)
        def _():
            self.run_in(k, 0).wait_send()

        @when(self.odd)
        def _():
            self.hand_on(5, 5, k, own, self.inward).wait_send()

        @when(self.odd, self.end)
        def _():
            self.over_chip(k, 0).wait_send()

        @when(self.odd, self.outer)
        def _():
            self.run_out(k, 0).wait_send()
            self.hand_on(6, 6, k, own, self.outward).wait_send()


STAGES = 10
BACK, GATHER, LEAVE, FINISH, WEIGH = range(STAGES, STAGES + 5)
LAGS = (0, 1, 3, 5, 7, 9, 11, 12, 14, 15)


def order(layout, chunks):
    early = sum(name in ("down", "up") for name, _, _, _ in layout.subs)
    back = [3 + 1.5 * index for index in range(chunks)]
    ready = back[-1] + 0.5
    items = [(at, 0, BACK, index) for index, at in enumerate(back)]
    items.append((ready - 0.02, 0, GATHER, 0))
    items += [(ready + 5, index, LEAVE, index) for index in range(chunks)]
    items += [(ready + 8 + index, 0, FINISH, index) for index in range(chunks)]
    for k in range(len(layout.subs)):
        at = k if k < early else max(early, ready) + k - early
        items.append((at - 0.01, 0, WEIGH, k))
        items += [(at + lag, STAGES - stage, stage, k) for stage, lag in enumerate(LAGS)]
    return [(step, index) for _, _, step, index in sorted(items)]


def layer_kernel(
    length_ref,
    tokens_hbm,
    wqkv_hbm,
    wout_hbm,
    gain_one_ref,
    bias_one_ref,
    wup_hbm,
    wdown_hbm,
    gain_two_ref,
    bias_two_ref,
    cot_hbm,
    out_hbm,
    grad_hbm,
    sums_hbm,
    tokens,
    cot,
    wqkv,
    wout,
    wup,
    wdown,
    packed,
    probs,
    attended,
    mine,
    theirs,
    unit_one,
    inv_one,
    normed,
    normed_low,
    slope,
    activated,
    grad_up_in,
    grad_res,
    grad_low,
    grad_att,
    grad_key,
    grad_val,
    grad_packed,
    small,
    parts,
    totals,
    near,
    across,
    inflow,
    middle,
    in_sem,
    out_sem,
    send_sem,
    recv_sem,
    sums_sem,
    sums_send,
    sums_recv,
    *,
    layout,
):
    rows, width = tokens.shape
    hidden = wup.shape[1]
    cols = wout.shape[0]
    pairs = cols // 128
    chunks = rows // CHUNK
    scaling = HEAD_DIM**-0.5
    other = {"tp": 1 - lax.axis_index("tp")}

    total = Sum(layout, parts, totals, near, across, inflow, middle, sums_send, sums_recv)
    barrier = pltpu.get_barrier_semaphore()
    pl.semaphore_signal(barrier, 1, device_id=other, device_id_type=MESH)
    total.greet(barrier)

    loads = [
        pltpu.make_async_copy(source, target, in_sem.at[place])
        for place, (source, target) in enumerate(
            (
                (tokens_hbm, tokens),
                (wqkv_hbm, wqkv),
                (wout_hbm, wout),
                (wup_hbm, wup),
                (wdown_hbm, wdown),
                (cot_hbm, cot),
            )
        )
    ]
    for load in loads:
        load.start()

    def at(index):
        return pl.ds(pl.multiple_of(index * CHUNK, CHUNK), CHUNK)

    def exchange(which, index):
        return pltpu.make_async_remote_copy(
            src_ref=mine.at[which, at(index)],
            dst_ref=theirs.at[which, at(index)],
            send_sem=send_sem.at[which, index],
            recv_sem=recv_sem.at[which, index],
            device_id=other,
            device_id_type=MESH,
        )

    def received(which, index):
        place = at(index)
        return mine[which, place, :].astype(F32) + theirs[which, place, :].astype(F32)

    small[...] = jnp.zeros_like(small)
    grad_key[...] = jnp.zeros_like(grad_key)
    grad_val[...] = jnp.zeros_like(grad_val)

    lane = lax.broadcasted_iota(jnp.int32, (1, 128), 1)
    first = jnp.where(lane < HEAD_DIM, 1.0, 0.0).astype(BF16)
    second = jnp.where(lane < HEAD_DIM, 0.0, 1.0).astype(BF16)
    live = lax.broadcasted_iota(jnp.int32, (1, rows), 1) < length_ref[0]

    def stacked(block):
        return jnp.concatenate([block * first, block * second], axis=0)

    def merged(both):
        return jnp.where(lane < HEAD_DIM, both[:CHUNK], both[CHUNK:])

    gain_one_row = gain_one_ref[...].reshape(1, width)
    bias_one_row = bias_one_ref[...].reshape(1, width)
    gain_two_row = gain_two_ref[...].reshape(1, width)
    bias_two_row = bias_two_ref[...].reshape(1, width)

    loads[0].wait()
    loads[1].wait()

    def project(index, carry):
        place = at(index)
        for part in range(3):
            value = dot(tokens[place, :], wqkv[part], 1, 0).astype(BF16)
            packed[part, place, :] = value * BF16(scaling) if part == 0 else value
        return carry

    lax.fori_loop(0, chunks, project, 0)
    loads[2].wait()
    total.meet(barrier, 1)

    def attend(index, carry):
        place = at(index)
        for pair in range(pairs):
            span = slice(pair * 128, pair * 128 + 128)
            scores = dot(stacked(packed[0, place, span]), packed[1, :, span], 1, 1)
            scores = jnp.where(live, scores, -1000000000.0)
            expo = jnp.exp(scores - jnp.max(scores, axis=-1, keepdims=True))
            weight = jnp.sum(expo, axis=-1, keepdims=True)
            low = (expo * (1.0 / weight)).astype(BF16)
            probs[pair * chunks + index] = low
            attended[place, span] = merged(dot(low, packed[2, :, span], 1, 0)).astype(BF16)
        mine[0, place, :] = dot(attended[place, :], wout[...], 1, 0).astype(BF16)
        exchange(0, index).start()
        return carry

    lax.fori_loop(0, chunks, attend, 0)
    loads[3].wait()
    loads[4].wait()
    loads[5].wait()

    def feed(index, carry):
        place = at(index)
        exchange(0, index).wait()
        unit, inverse = norm_forward(tokens[place, :].astype(F32) + received(0, index))
        unit_one[place, :] = unit
        inv_one[place, :] = inverse
        value = unit * gain_one_row + bias_one_row
        normed[place, :] = value
        normed_low[place, :] = value.astype(BF16)
        for start in range(0, hidden, SUB):
            span = slice(start, start + SUB)
            upward = dot(normed_low[place, :], wup[:, span], 1, 0)
            share = 0.5 + 0.5 * lax.erf(upward * 0.7071067811865476)
            activated[place, span] = (upward * share).astype(BF16)
            slope[place, span] = share + upward * jnp.exp(upward * upward * -0.5) * 0.3989422804014327
        mine[1, place, :] = dot(activated[place, :], wdown[...], 1, 0).astype(BF16)
        exchange(1, index).start()
        return carry

    lax.fori_loop(0, chunks, feed, 0)

    def turn(index, carry):
        place = at(index)
        exchange(1, index).wait()
        unit, inverse = norm_forward(normed[place, :] + received(1, index))
        mine[4, place, :] = (unit * gain_two_row + bias_two_row).astype(BF16)
        pltpu.make_async_copy(mine.at[4, place], out_hbm.at[place], out_sem.at[0, index]).start()
        flow = cot[place, :].astype(F32)
        small[2:3, :] += jnp.sum(flow * unit, axis=0, keepdims=True)
        small[3:4, :] += jnp.sum(flow, axis=0, keepdims=True)
        grad = norm_backward(flow * gain_two_row, unit, inverse)
        grad_res[place, :] = grad
        grad_low[0, place, :] = grad.astype(BF16)
        for start in range(0, hidden, SUB):
            span = slice(start, start + SUB)
            grad_act = dot(grad_low[0, place, :], wdown[span, :], 1, 1)
            grad_up_in[place, span] = (grad_act * slope[place, span]).astype(BF16)
        mine[2, place, :] = dot(grad_up_in[place, :], wup[...], 1, 1).astype(BF16)
        exchange(2, index).start()
        return carry

    lax.fori_loop(0, chunks, turn, 0)

    def attend_back(index):
        place = at(index)
        exchange(2, index).wait()
        unit = unit_one[place, :]
        flow = grad_res[place, :] + received(2, index)
        small[0:1, :] += jnp.sum(flow * unit, axis=0, keepdims=True)
        small[1:2, :] += jnp.sum(flow, axis=0, keepdims=True)
        grad = norm_backward(flow * gain_one_row, unit, inv_one[place, :])
        grad_res[place, :] = grad
        grad_low[1, place, :] = grad.astype(BF16)
        grad_att[place, :] = dot(grad_low[1, place, :], wout[...], 1, 1).astype(BF16)
        for pair in range(pairs):
            span = slice(pair * 128, pair * 128 + 128)
            low = probs[pair * chunks + index]
            pull = stacked(grad_att[place, span])
            seen = attended[place, span].astype(F32)
            centre = jnp.sum(
                pull.astype(F32) * jnp.concatenate([seen, seen], axis=0), axis=-1, keepdims=True
            )
            grad_probs = dot(pull, packed[2, :, span], 1, 1)
            grad_scores = (low.astype(F32) * (grad_probs - centre)).astype(BF16)
            grad_val[:, span] += dot(low, pull, 0, 0)
            grad_key[:, span] += dot(grad_scores, stacked(packed[0, place, span]), 0, 0)
            grad_query = merged(dot(grad_scores, packed[1, :, span], 1, 0)) * scaling
            grad_packed[0, place, span] = grad_query.astype(BF16)

    def gather():
        grad_packed[1] = grad_key[...].astype(BF16)
        grad_packed[2] = grad_val[...].astype(BF16)

    def leave(index):
        place = at(index)
        value = dot(grad_packed[0, place, :], wqkv[0], 1, 1)
        value += dot(grad_packed[1, place, :], wqkv[1], 1, 1)
        value += dot(grad_packed[2, place, :], wqkv[2], 1, 1)
        mine[3, place, :] = value.astype(BF16)
        exchange(3, index).start()

    def weigh(k):
        name, which, start, extent = layout.subs[k]
        if name == "down":
            rows_at = which * SUB
            value = dot(activated[:, rows_at : rows_at + SUB], grad_low[0], 0, 0)
            parts[start : start + SUB, :] = value.astype(BF16)
        if name == "up":
            rows_at, cols_at = which % 2 * SUB, which // 2 * width
            left = normed_low[:, rows_at : rows_at + SUB]
            value = dot(left, grad_up_in[:, cols_at : cols_at + width], 0, 0)
            parts[start : start + SUB, :] = value.astype(BF16)
        if name == "out":
            parts[start : start + SUB, :] = dot(attended[...], grad_low[1], 0, 0).astype(BF16)
            parts[start + SUB : start + extent, :] = small[...].astype(BF16)
        if name == "qkv":
            span = slice(which * 128, which * 128 + 128)
            for part in range(3):
                value = dot(tokens[...], grad_packed[part, :, span], 0, 0).astype(BF16)
                for side in range(2):
                    left = side * SUB + part * 128
                    rows_at = side * SUB
                    parts[start : start + SUB, left : left + 128] = value[rows_at : rows_at + SUB]

    def finish(index):
        place = at(index)
        exchange(3, index).wait()
        mine[5, place, :] = (grad_res[place, :] + received(3, index)).astype(BF16)
        pltpu.make_async_copy(mine.at[5, place], grad_hbm.at[place], out_sem.at[1, index]).start()

    def store(k):
        _, _, start, extent = layout.subs[k]
        place = pl.ds(start, extent)
        return pltpu.make_async_copy(totals.at[place], sums_hbm.at[place], sums_sem.at[k])

    for step, index in order(layout, chunks):
        if step == BACK:
            attend_back(index)
        elif step == GATHER:
            gather()
        elif step == LEAVE:
            leave(index)
        elif step == FINISH:
            finish(index)
        elif step == WEIGH:
            weigh(index)
        else:
            total.stage(step, index)
            if step == STAGES - 1:
                store(index).start()

    for index in range(chunks):
        place = at(index)
        pltpu.make_async_copy(mine.at[4, place], out_hbm.at[place], out_sem.at[0, index]).wait()
        pltpu.make_async_copy(mine.at[5, place], grad_hbm.at[place], out_sem.at[1, index]).wait()
    for k in range(len(layout.subs)):
        total.settle(k)
        store(k).wait()


def widen_kernel(
    sums_hbm,
    out_in,
    grad_in,
    out_hbm,
    grad_hbm,
    qkv_hbm,
    wout_hbm,
    gain_one_hbm,
    bias_one_hbm,
    up_hbm,
    down_hbm,
    gain_two_hbm,
    bias_two_hbm,
    sums,
    wide,
    vectors,
    rows_in,
    in_sem,
    out_sem,
    row_sem,
    *,
    layout,
):
    slots = wide.shape[0]
    width = sums.shape[1]

    def load(k):
        _, _, start, rows = layout.subs[k]
        return pltpu.make_async_copy(
            sums_hbm.at[pl.ds(start, rows)], sums.at[pl.ds(start, rows)], in_sem.at[k]
        )

    def stores(k):
        name, which, _, _ = layout.subs[k]
        slot = k % slots
        block = wide.at[slot, pl.ds(0, SUB)]
        if name == "down":
            pieces = [(block, down_hbm.at[pl.ds(which * SUB, SUB)])]
        elif name == "up":
            pieces = [
                (block, up_hbm.at[pl.ds(which % 2 * SUB, SUB), pl.ds(which // 2 * width, width)])
            ]
        elif name == "out":
            pieces = [(block, wout_hbm)]
            for row, target in enumerate((gain_one_hbm, bias_one_hbm, gain_two_hbm, bias_two_hbm)):
                pieces.append((vectors.at[row], target))
        else:
            pieces = [
                (
                    wide.at[slot, pl.ds(0, SUB), pl.ds(half * SUB + part * 128, 128)],
                    qkv_hbm.at[part, pl.ds(half * SUB, SUB), pl.ds(which * 128, 128)],
                )
                for half in range(2)
                for part in range(3)
            ]
        return [
            pltpu.make_async_copy(source, target, out_sem.at[slot, place])
            for place, (source, target) in enumerate(pieces)
        ]

    through = ((out_in, out_hbm), (grad_in, grad_hbm))
    for place, (source, _) in enumerate(through):
        pltpu.make_async_copy(source, rows_in.at[place], row_sem.at[place]).start()
    for k in range(len(layout.subs)):
        load(k).start()
    for place, (source, target) in enumerate(through):
        pltpu.make_async_copy(source, rows_in.at[place], row_sem.at[place]).wait()
        pltpu.make_async_copy(rows_in.at[place], target, row_sem.at[2 + place]).start()
    for k, (name, _, start, _) in enumerate(layout.subs):
        load(k).wait()
        if k >= slots:
            for store in stores(k - slots):
                store.wait()
        wide[k % slots, 0:SUB, :] = sums[start : start + SUB, :].astype(F32)
        if name == "out":
            low = sums[start + SUB : start + SUB + 16, :].astype(F32)
            for row in range(4):
                vectors[row] = low[row]
        for store in stores(k):
            store.start()
    for k in range(len(layout.subs) - slots, len(layout.subs)):
        for store in stores(k):
            store.wait()
    for place, (_, target) in enumerate(through):
        pltpu.make_async_copy(rows_in.at[place], target, row_sem.at[2 + place]).wait()


def on_device(
    tokens,
    lengths,
    weight_qkv,
    weight_out,
    gain_one,
    bias_one,
    weight_up,
    weight_down,
    gain_two,
    bias_two,
    cotangent,
):
    seq_count, rows, width = tokens.shape
    cols, hidden = weight_out.shape[0], weight_up.shape[1]
    assert seq_count == 1 and rows % CHUNK == 0 and lax.axis_size("tp") == 2
    layout = Layout(width, cols, hidden)
    count = len(layout.subs)
    chunks = rows // CHUNK
    pairs = cols // 128
    whole = pl.BlockSpec(memory_space=pltpu.VMEM)
    out_rows, grad_rows, sums = pl.pallas_call(
        functools.partial(layer_kernel, layout=layout),
        name="layer",
        out_shape=(
            jax.ShapeDtypeStruct((rows, width), BF16),
            jax.ShapeDtypeStruct((rows, width), BF16),
            jax.ShapeDtypeStruct((layout.rows, width), BF16),
        ),
        in_specs=[
            pl.BlockSpec(memory_space=pltpu.SMEM),
            ANY,
            ANY,
            ANY,
            whole,
            whole,
            ANY,
            ANY,
            whole,
            whole,
            ANY,
        ],
        out_specs=(ANY, ANY, ANY),
        scratch_shapes=[
            pltpu.VMEM((rows, width), BF16),
            pltpu.VMEM((rows, width), BF16),
            pltpu.VMEM((3, width, cols), BF16),
            pltpu.VMEM((cols, width), BF16),
            pltpu.VMEM((width, hidden), BF16),
            pltpu.VMEM((hidden, width), BF16),
            pltpu.VMEM((3, rows, cols), BF16),
            pltpu.VMEM((pairs * chunks, 2 * CHUNK, rows), BF16),
            pltpu.VMEM((rows, cols), BF16),
            pltpu.VMEM((6, rows, width), BF16),
            pltpu.VMEM((4, rows, width), BF16),
            pltpu.VMEM((rows, width), F32),
            pltpu.VMEM((rows, 1), F32),
            pltpu.VMEM((rows, width), F32),
            pltpu.VMEM((rows, width), BF16),
            pltpu.VMEM((rows, hidden), F32),
            pltpu.VMEM((rows, hidden), BF16),
            pltpu.VMEM((rows, hidden), BF16),
            pltpu.VMEM((rows, width), F32),
            pltpu.VMEM((2, rows, width), BF16),
            pltpu.VMEM((rows, cols), BF16),
            pltpu.VMEM((rows, cols), F32),
            pltpu.VMEM((rows, cols), F32),
            pltpu.VMEM((3, rows, cols), BF16),
            pltpu.VMEM((SMALL, width), F32),
            pltpu.VMEM((layout.rows, width), BF16),
            pltpu.VMEM((layout.rows, width), BF16),
            pltpu.VMEM((layout.rows // 2, width), BF16),
            pltpu.VMEM((layout.rows // 4, width), BF16),
            pltpu.VMEM((layout.rows // 4, width), BF16),
            pltpu.VMEM((layout.rows // 4, width), BF16),
            pltpu.SemaphoreType.DMA((6,)),
            pltpu.SemaphoreType.DMA((2, chunks)),
            pltpu.SemaphoreType.DMA((4, chunks)),
            pltpu.SemaphoreType.DMA((4, chunks)),
            pltpu.SemaphoreType.DMA((count,)),
            pltpu.SemaphoreType.DMA((8, count)),
            pltpu.SemaphoreType.DMA((8, count)),
        ],
        compiler_params=pltpu.CompilerParams(
            collective_id=1, has_side_effects=True, vmem_limit_bytes=VMEM_LIMIT
        ),
    )(
        lengths,
        tokens.reshape(rows, width),
        jnp.transpose(weight_qkv, (1, 0, 2)),
        weight_out,
        gain_one,
        bias_one,
        weight_up,
        weight_down,
        gain_two,
        bias_two,
        cotangent.reshape(rows, width),
    )
    vector = jax.ShapeDtypeStruct((width,), F32)
    results = pl.pallas_call(
        functools.partial(widen_kernel, layout=layout),
        name="widen",
        out_shape=(
            jax.ShapeDtypeStruct((rows, width), BF16),
            jax.ShapeDtypeStruct((rows, width), BF16),
            jax.ShapeDtypeStruct((3, width, cols), F32),
            jax.ShapeDtypeStruct((cols, width), F32),
            vector,
            vector,
            jax.ShapeDtypeStruct((width, hidden), F32),
            jax.ShapeDtypeStruct((hidden, width), F32),
            vector,
            vector,
        ),
        in_specs=[ANY] * 3,
        out_specs=(ANY,) * 10,
        scratch_shapes=[
            pltpu.VMEM((layout.rows, width), BF16),
            pltpu.VMEM((4, SUB, width), F32),
            pltpu.VMEM((4, width), F32),
            pltpu.VMEM((2, rows, width), BF16),
            pltpu.SemaphoreType.DMA((count,)),
            pltpu.SemaphoreType.DMA((4, 6)),
            pltpu.SemaphoreType.DMA((4,)),
        ],
        compiler_params=pltpu.CompilerParams(vmem_limit_bytes=VMEM_LIMIT),
    )(sums, out_rows, grad_rows)
    return (
        results[0].reshape(seq_count, rows, width),
        results[1].reshape(seq_count, rows, width),
        jnp.transpose(results[2], (1, 0, 2)),
        results[3],
        results[4],
        results[5],
        results[6],
        results[7],
        results[8],
        results[9],
    )


def solution(mesh):
    batch = P(("dp", "dq"), None, None)
    return jax.shard_map(
        on_device,
        mesh=mesh,
        in_specs=(
            batch,
            P(("dp", "dq")),
            P(None, None, "tp"),
            P("tp", None),
            P(),
            P(),
            P(None, "tp"),
            P("tp", None),
            P(),
            P(),
            batch,
        ),
        out_specs=(
            batch,
            batch,
            P(None, None, "tp"),
            P("tp", None),
            P(),
            P(),
            P(None, "tp"),
            P("tp", None),
            P(),
            P(),
        ),
        check_vma=False,
    )
```

time: 195 us -> 145 us (0.74)
  Pallas kernels: 182 us -> 143 us
  other arithmetic: 5.14 us -> 0 us
  local copies, waits for them, and re-layouts: 5.07 us -> 0 us
    pallas_call x1 -> x0, Pallas kernels: 92.1 us -> none  [on_device(): pl.pallas_call(functools.partial(sum_kernel, layout=layout), name='sum',...]
    pallas_call x1, Pallas kernels: 81.3 us -> 134 us  [on_device(): pl.pallas_call(functools.partial(layer_kernel, layout=layout), name='laye...]
    pallas_call x4 -> x0, other arithmetic: 5.14 us -> none  [on_device(): pl.pallas_call(functools.partial(widen_kernel, layout=layout), name='wide...]
    reshape x4 -> x0, local copies, waits for them, and re-layouts: 5.07 us -> none  [the longest x1 1.27 us: on_device(): gain_one.reshape(1, width)]
where the time goes in v2:
time: 145 us
  Pallas kernels  143 us (99%)
  between operations  1.48 us (1%)
    pallas_call x1, Pallas kernels, on_device(): pl.pallas_call(functools.partial(layer_kernel, layout=layout), name='laye...  134 us
    pallas_call x1, Pallas kernels, on_device(): pl.pallas_call(functools.partial(widen_kernel, layout=layout), name='wide...  8.93 us

profile of v2, /device:TPU:0, one launch (start us, length us, event | category | flops | bytes accessed | tf_op | source)
XLA Modules:
  0.0 144.7 jit_solution(16705970626397368438)
XLA Ops:
  1.3 134.3 %layer.1 = (bf16[512,768]{1,0:T(8,128)(2,1)}, bf16[512,768]{1,0:T(8,128)(2,1)}, bf16[4672,768]{1,0:T(8,128)(2,1)}) custom-call(s32[1]{0:T(128)S(6)} %copy.21.length_ref, bf16[512,768]{1,0:T(8,128)(2,1)} %bitcast.7, bf16[3,768,384]{2,1,0:T(8,128)(2,1)} %bitcast.6, bf16[384,768]{1,0:T(8,128)(2,1)} %wout_hbm.1, f32[768]{0:T(1024)} %gain_one_ref.1, ...), custom_call_target="tpu_custom_call" | custom-call | tf_op jit(solution)/shard_map/layer/pallas_call | solution.py:756
  135.6 8.9 %widen.1 = (bf16[512,768]{1,0:T(8,128)(2,1)}, bf16[512,768]{1,0:T(8,128)(2,1)}, f32[3,768,384]{2,1,0:T(8,128)}, f32[384,768]{1,0:T(8,128)}, f32[768]{0:T(1024)},...) custom-call(bf16[4672,768]{1,0:T(8,128)(2,1)} %get-tuple-element.23.sums_hbm, ...), custom_call_target="tpu_custom_call" | custom-call | tf_op jit(solution)/shard_map/widen/pallas_call | solution.py:835
